TPU v7x, 32 devices: a whole 2x2x4 slice. The times are simulated.
32 devices in a mesh: tm: 8 (over y, x, core), panel: 4 (over z).
Axes of the slice: x: 2, y: 2, z: 4, core: 2. Of those that a mesh axis runs over, the one named last changes fastest.
Arguments:
- series: float32 [48, 2048], P(None, 'tm'), may hold values from -20 to 20, as said below
- start_block: float32 [18432, 64], P(('tm', 'panel')), may hold values from -6 to 6
Outputs:
- covariance: float32 [18432, 18432], P(('tm', 'panel'))
- basis: float32 [7, 18432, 64], P(None, ('tm', 'panel'))
- diag_blocks: float32 [6, 64, 64], replicated
- off_blocks: float32 [7, 64, 64], replicated
Inputs may be any that keep to these rules, and one draw needn't show every extreme that they name: `series`: each channel has its own scale.
All inputs are finite; a program needn't handle non-finite values.
Results may differ from a plain program's by a relative error of at most 0.0003.
Values sent between devices are 32-bit elements; how exact they have to be, the bound alone decides.
A program may use at most 192 MiB of HBM per device.

v0:
```python
import jax
import jax.numpy as jnp
from jax import lax
from jax.experimental import pallas as pl
from jax.experimental.pallas import tpu as pltpu
from jax.sharding import PartitionSpec as P

M = 384
ITERS = 6


exact_precision = lax.Precision.HIGHEST


def passed_along(block, axis, distance):
    devices = range(lax.axis_size(axis))
    route = [(i - distance, i) for i in devices if i - distance in devices]
    return lax.ppermute(block, axis, route)


def lag_kernel(x_ref, g_ref, o_ref):
    groups, _, width = g_ref.shape
    depth = x_ref.shape[1] // groups
    x = x_ref[...]
    for step in range(o_ref.shape[1] // width):
        window = g_ref[:, step : step + depth, :].reshape(groups * depth, width)
        o_ref[:, step * width : (step + 1) * width] = jnp.dot(
            x, window, precision=exact_precision, preferred_element_type=jnp.float32
        )


def lag_products(local_rows, extended):
    channels, day_count = local_rows.shape
    groups = 8
    width = groups * channels
    depth = day_count // groups
    rows = depth + M // groups
    days = jnp.pad(extended, ((0, 0), (0, max(0, rows * groups + groups - extended.shape[1]))))
    flat = days.T.reshape(-1)
    shifted = jnp.stack(
        [
            lax.slice(flat, (r * channels,), (r * channels + rows * width,)).reshape(rows, width)
            for r in range(groups)
        ]
    )
    by_group = local_rows.reshape(channels, depth, groups).transpose(0, 2, 1)
    return pl.pallas_call(
        lag_kernel,
        out_shape=jax.ShapeDtypeStruct((channels, M * channels), jnp.float32),
        in_specs=[pl.BlockSpec(memory_space=pltpu.VMEM)] * 2,
        out_specs=pl.BlockSpec(memory_space=pltpu.VMEM),
    )(by_group.reshape(channels, day_count), shifted)


def gram_kernel(sizes, q_ref, w_ref, o_ref, held, arrived, send_sem, recv_sem):
    partners = []
    for axis, size in sizes:
        me = lax.axis_index(axis)
        distance = 1
        while distance < size:
            partners.append((axis, me + distance - 2 * distance * ((me // distance) % 2)))
            distance *= 2
    barrier = pltpu.get_barrier_semaphore()
    for axis, other in partners:
        pl.semaphore_signal(
            barrier, inc=1, device_id={axis: other}, device_id_type=pl.DeviceIdType.MESH
        )
    both = jnp.concatenate([q_ref[...], w_ref[...]], axis=1)
    held[0] = lax.dot_general(
        both,
        both,
        (((0,), (0,)), ((), ())),
        precision=exact_precision,
        preferred_element_type=jnp.float32,
    )
    pl.semaphore_wait(barrier, len(partners))
    for step, (axis, other) in enumerate(partners):
        copy = pltpu.make_async_remote_copy(
            src_ref=held.at[step],
            dst_ref=arrived.at[step],
            send_sem=send_sem.at[step],
            recv_sem=recv_sem.at[step],
            device_id={axis: other},
            device_id_type=pl.DeviceIdType.MESH,
        )
        copy.start()
        copy.wait()
        held[step + 1] = held[step] + arrived[step]
    o_ref[...] = held[len(partners)]


def grams(q, w):
    sizes = [("tm", lax.axis_size("tm")), ("panel", lax.axis_size("panel"))]
    steps = sum(size.bit_length() - 1 for _, size in sizes)
    width = q.shape[1] + w.shape[1]
    out = pl.pallas_call(
        lambda *refs: gram_kernel(sizes, *refs),
        out_shape=jax.ShapeDtypeStruct((width, width), jnp.float32),
        in_specs=[pl.BlockSpec(memory_space=pltpu.VMEM)] * 2,
        out_specs=pl.BlockSpec(memory_space=pltpu.VMEM),
        scratch_shapes=[
            pltpu.VMEM((steps + 1, width, width), jnp.float32),
            pltpu.VMEM((steps, width, width), jnp.float32),
            pltpu.SemaphoreType.DMA((steps,)),
            pltpu.SemaphoreType.DMA((steps,)),
        ],
        compiler_params=pltpu.CompilerParams(collective_id=0, has_side_effects=True),
    )(q, w)
    half = q.shape[1]
    return out[:half, :half], out[:half, half:], out[half:, half:]


def local(series, start_block):
    channels, day_count = series.shape
    tm_size = lax.axis_size("tm")
    panel_size = lax.axis_size("panel")
    total_days = day_count * tm_size
    reach_hops = (M - 1 + day_count - 1) // day_count
    pieces = [series]
    moving = series
    for distance in range(reach_hops):
        moving = passed_along(moving, "tm", -1)
        pieces.append(moving)
    extended = jnp.concatenate(pieces, axis=1)
    summed = lax.psum(lag_products(series, extended), "tm")
    counts = (total_days - jnp.arange(M)).astype(jnp.float32)
    counts = (total_days - jnp.arange(M * channels) // channels).astype(jnp.float32)
    normed = summed / counts[None, :]
    blocks = normed.reshape(channels, M, channels)
    before = jnp.transpose(blocks, (2, 1, 0))[:, :0:-1, :].reshape(channels, (M - 1) * channels)
    two_sided = jnp.concatenate([before, normed], axis=1)
    lags_here = M // (tm_size * panel_size)
    block_index = lax.axis_index("tm") * panel_size + lax.axis_index("panel")
    first = (M - lags_here - block_index * lags_here) * channels
    near = lax.dynamic_slice(
        two_sided, (jnp.int32(0), first), (channels, (M + lags_here - 1) * channels)
    )
    row_list = []
    for offset in range(lags_here):
        start = (lags_here - 1 - offset) * channels
        row_list.append(near[:, start : start + M * channels])
    covariance = jnp.concatenate(row_list, axis=0)

    factor = jnp.linalg.cholesky(grams(start_block, start_block)[0])
    current = jax.scipy.linalg.solve_triangular(factor, start_block.T, lower=True).T
    previous = jnp.zeros_like(current)
    upper = factor.T
    basis_list = [current]
    diagonal_list = []
    upper_list = [upper]
    for iteration in range(ITERS):
        work = jnp.dot(
            covariance,
            lax.all_gather(current, ("tm", "panel"), axis=0, tiled=True),
            precision=lax.Precision.HIGH,
            preferred_element_type=jnp.float32,
        )
        if iteration > 0:
            work = work - jnp.dot(
                previous, upper.T, precision=exact_precision, preferred_element_type=jnp.float32
            )
        basis_gram, diagonal, work_gram = grams(current, work)
        work = work - jnp.dot(
            current, diagonal, precision=exact_precision, preferred_element_type=jnp.float32
        )
        cross_term = jnp.dot(
            diagonal.T, diagonal, precision=exact_precision, preferred_element_type=jnp.float32
        )
        weighted = jnp.dot(
            diagonal.T,
            jnp.dot(
                basis_gram, diagonal, precision=exact_precision, preferred_element_type=jnp.float32
            ),
            precision=exact_precision,
            preferred_element_type=jnp.float32,
        )
        gram_matrix = work_gram - 2.0 * cross_term + weighted
        factor = jnp.linalg.cholesky(gram_matrix)
        upper = factor.T
        previous = current
        current = jax.scipy.linalg.solve_triangular(factor, work.T, lower=True).T
        basis_list.append(current)
        diagonal_list.append(diagonal)
        upper_list.append(upper)
    return (covariance, jnp.stack(basis_list), jnp.stack(diagonal_list), jnp.stack(upper_list))


def solution(mesh):
    placed = (P(None, "tm"), P(("tm", "panel"), None))
    return jax.shard_map(
        local,
        mesh=mesh,
        in_specs=placed,
        out_specs=(P(("tm", "panel"), None), P(None, ("tm", "panel"), None), P(), P()),
        check_vma=False,
    )
```

profile of v0, /device:TPU:0, one launch (start us, length us, event | category | flops | bytes accessed | tf_op | source)
XLA Modules:
  0.0 1074.0 jit_solution(13053450079170921308)
XLA Ops:
  22.4 11.8 %shard_map.57 = f32[48,18432]{1,0:T(8,128)} custom-call(f32[48,256]{1,0:T(8,128)} %reshape.61.x_ref, f32[8,80,384]{2,1,0:T(8,128)} %copy-done.18), custom_call_target="tpu_custom_call" | custom-call | tf_op jit(solution)/shard_map/pallas_call | solution.py:47
  35.7 26.3 %shard_map.58 = f32[128,128]{1,0:T(8,128)} custom-call(f32[576,64]{1,0:T(8,128)} %copy.280.refs_0_.refs_1_, f32[576,64]{1,0:T(8,128)} %copy.280.refs_0_.refs_1_), custom_call_target="tpu_custom_call" | custom-call | tf_op jit(solution)/shard_map/pallas_call | solution.py:96
  77.8 41.9 %all-reduce.2.cloned.1.call-done = f32[48,18432]{1,0:T(8,128)} async-done(((f32[48,18432]{1,0:T(8,128)}), f32[48,18432]{1,0:T(8,128)}) %all-reduce.2.cloned.1.call-update) | async-done | bytes 3538960 | tf_op jit(solution)/shard_map/psum | solution.py:125
  128.2 8.5 slice.184
  136.6 74.3 %rev.3 = f32[48,383,48]{0,1,2:T(8,128)} reverse(f32[48,383,48]{0,1,2:T(8,128)} %slice.184), dimensions={1} | reverse | bytes 7059456 | tf_op jit(solution)/shard_map/rev | solution.py:130
  211.0 12.4 %copy.279 = f32[48,383,48]{2,1,0:T(8,128)} copy(f32[48,383,48]{0,1,2:T(8,128)} %rev.3) | data formatting | bytes 7059456 | tf_op jit(solution)/shard_map/rev | solution.py:130
  223.3 10.4 reshape.63
  268.3 8.0 copy.286
  282.8 24.6 %fusion.97 = f32[576,64]{0,1:T(8,128)S(1)} fusion(f32[576,18432]{1,0:T(8,128)} %slice_dynamic-update-slice_fusion, f32[18432,64]{0,1:T(8,128)} %reshape.65), kind=kOutput, calls=%fused_computation.204 | convolution fusion | flops 4076863488 | bytes 47333376 | tf_op jit(solution)/shard_map/dot_general | solution.py:152
  308.2 21.1 %shard_map.59 = f32[128,128]{1,0:T(8,128)} custom-call(f32[576,64]{1,0:T(8,128)} %bitcast.203, f32[576,64]{1,0:T(8,128)} %copy.287.refs_1_), custom_call_target="tpu_custom_call" | custom-call | tf_op jit(solution)/shard_map/pallas_call | solution.py:96
  348.7 62.9 %all-gather.15.cloned.1.call-done = f32[32,576,64]{1,2,0:T(8,128)} async-done(((f32[1,576,64]{1,2,0:T(8,128)}), f32[32,576,64]{1,2,0:T(8,128)}) %all-gather.15.cloned.1.call-update) | async-done | bytes 4718608 | tf_op jit(solution)/shard_map/all_gather | solution.py:154
  411.6 7.8 copy.294
  419.4 6.4 reshape.67
  425.8 24.6 %fusion.98 = f32[576,64]{0,1:T(8,128)S(1)} fusion(f32[576,18432]{1,0:T(8,128)} %slice_dynamic-update-slice_fusion, f32[18432,64]{0,1:T(8,128)} %reshape.67), kind=kOutput, calls=%fused_computation.205 | convolution fusion | flops 4076863488 | bytes 47333376 | tf_op jit(solution)/shard_map/dot_general | solution.py:152
  452.2 19.4 %shard_map.60 = f32[128,128]{1,0:T(8,128)} custom-call(f32[576,64]{1,0:T(8,128)} %bitcast.205, f32[576,64]{1,0:T(8,128)} %copy.295.refs_1_), custom_call_target="tpu_custom_call" | custom-call | tf_op jit(solution)/shard_map/pallas_call | solution.py:96
  490.8 63.4 %all-gather.17.cloned.1.call-done = f32[32,576,64]{1,2,0:T(8,128)} async-done(((f32[1,576,64]{1,2,0:T(8,128)}), f32[32,576,64]{1,2,0:T(8,128)}) %all-gather.17.cloned.1.call-update) | async-done | bytes 4718608 | tf_op jit(solution)/shard_map/all_gather | solution.py:154
  554.2 7.8 copy.302
  568.4 24.6 %fusion.99 = f32[576,64]{0,1:T(8,128)S(1)} fusion(f32[576,18432]{1,0:T(8,128)} %slice_dynamic-update-slice_fusion, f32[18432,64]{0,1:T(8,128)} %reshape.69), kind=kOutput, calls=%fused_computation.206 | convolution fusion | flops 4076863488 | bytes 47333376 | tf_op jit(solution)/shard_map/dot_general | solution.py:152
  594.9 19.4 %shard_map.61 = f32[128,128]{1,0:T(8,128)} custom-call(f32[576,64]{1,0:T(8,128)} %bitcast.207, f32[576,64]{1,0:T(8,128)} %copy.303.refs_1_), custom_call_target="tpu_custom_call" | custom-call | tf_op jit(solution)/shard_map/pallas_call | solution.py:96
  633.3 63.3 %all-gather.19.cloned.1.call-done = f32[32,576,64]{1,2,0:T(8,128)} async-done(((f32[1,576,64]{1,2,0:T(8,128)}), f32[32,576,64]{1,2,0:T(8,128)}) %all-gather.19.cloned.1.call-update) | async-done | bytes 4718608 | tf_op jit(solution)/shard_map/all_gather | solution.py:154
  696.7 7.8 copy.310
  710.9 24.6 %fusion.100 = f32[576,64]{0,1:T(8,128)S(1)} fusion(f32[576,18432]{1,0:T(8,128)} %slice_dynamic-update-slice_fusion, f32[18432,64]{0,1:T(8,128)} %reshape.71), kind=kOutput, calls=%fused_computation.207 | convolution fusion | flops 4076863488 | bytes 47333376 | tf_op jit(solution)/shard_map/dot_general | solution.py:152
  737.3 19.4 %shard_map.62 = f32[128,128]{1,0:T(8,128)} custom-call(f32[576,64]{1,0:T(8,128)} %bitcast.209, f32[576,64]{1,0:T(8,128)} %copy.311.refs_1_), custom_call_target="tpu_custom_call" | custom-call | tf_op jit(solution)/shard_map/pallas_call | solution.py:96
  775.9 63.2 %all-gather.21.cloned.1.call-done = f32[32,576,64]{1,2,0:T(8,128)} async-done(((f32[1,576,64]{1,2,0:T(8,128)}), f32[32,576,64]{1,2,0:T(8,128)}) %all-gather.21.cloned.1.call-update) | async-done | bytes 4718608 | tf_op jit(solution)/shard_map/all_gather | solution.py:154
  839.1 7.8 copy.318
  846.9 6.4 reshape.73
  853.3 24.8 %fusion.101 = f32[576,64]{0,1:T(8,128)S(1)} fusion(f32[576,18432]{1,0:T(8,128)} %slice_dynamic-update-slice_fusion, f32[18432,64]{0,1:T(8,128)} %reshape.73), kind=kOutput, calls=%fused_computation.208 | convolution fusion | flops 4076863488 | bytes 47333376 | tf_op jit(solution)/shard_map/dot_general | solution.py:152
  880.1 19.4 %shard_map.63 = f32[128,128]{1,0:T(8,128)} custom-call(f32[576,64]{1,0:T(8,128)} %bitcast.211, f32[576,64]{1,0:T(8,128)} %copy.319.refs_1_), custom_call_target="tpu_custom_call" | custom-call | tf_op jit(solution)/shard_map/pallas_call | solution.py:96
  927.2 54.9 %all-gather.23.cloned.1.call-done = f32[32,576,64]{1,2,0:T(8,128)} async-done(((f32[1,576,64]{1,2,0:T(8,128)}), f32[32,576,64]{1,2,0:T(8,128)}) %all-gather.23.cloned.1.call-update) | async-done | bytes 4718608 | tf_op jit(solution)/shard_map/all_gather | solution.py:154
  982.1 7.9 copy.326
  996.2 24.8 %fusion.102 = f32[576,64]{0,1:T(8,128)S(1)} fusion(f32[576,18432]{1,0:T(8,128)} %slice_dynamic-update-slice_fusion, f32[18432,64]{0,1:T(8,128)} %reshape.75), kind=kOutput, calls=%fused_computation.209 | convolution fusion | flops 4076863488 | bytes 47333376 | tf_op jit(solution)/shard_map/dot_general | solution.py:152
  1022.8 19.4 %shard_map.64 = f32[128,128]{1,0:T(8,128)} custom-call(f32[576,64]{1,0:T(8,128)} %bitcast.213, f32[576,64]{1,0:T(8,128)} %copy.327.refs_1_), custom_call_target="tpu_custom_call" | custom-call | tf_op jit(solution)/shard_map/pallas_call | solution.py:96
  (252 shorter events, 238.2 us)
Async XLA Ops:
  8.0 111.7 %all-reduce.2.cloned.1.call-start = ((), (), s32[]{:S(2)}) async-start(), calls=%async_computation | async-start | bytes 7077888 | tf_op jit(solution)/shard_map/psum | solution.py:125
  8.0 3.3 collective-permute-start
  11.4 6.2 collective-permute-start.1
  21.4 13.4 %copy-start.19 = (f32[576,64]{0,1:T(8,128)S(1)}, f32[576,64]{0,1:T(8,128)}, u32[]{:S(2)}) copy-start(f32[576,64]{0,1:T(8,128)} %param.6) | copy-start | bytes 442372
  21.5 0.9 copy-start.18
  34.3 234.1 %all-gather.13.cloned.1.call-start = ((), (), s32[]{:S(2)}) async-start(), calls=%async_computation.1 | async-start | bytes 5406720 | tf_op jit(solution)/shard_map/all_gather | solution.py:154
  69.5 6.3 copy-start.20
  76.1 1.7 copy-start.11
  76.3 1.5 copy-start
  77.1 334.5 %all-gather.15.cloned.1.call-start = ((), (), s32[]{:S(2)}) async-start(), calls=%async_computation.2 | async-start | bytes 5406720 | tf_op jit(solution)/shard_map/all_gather | solution.py:154
  282.8 48.5 %copy-start.12 = (f32[64,576]{1,0:T(8,128)S(1)}, f32[64,576]{1,0:T(8,128)}, u32[]{:S(2)}) copy-start(f32[64,576]{1,0:T(8,128)} %copy-done.11) | copy-start | bytes 442372
  347.3 72.1 %copy-start.2 = (f32[64,576]{0,1:T(8,128)}, f32[64,576]{0,1:T(8,128)S(1)}, u32[]{:S(2)}) copy-start(f32[64,576]{0,1:T(8,128)S(1)} %copy.292) | copy-start | bytes 442372
  348.2 206.0 %all-gather.17.cloned.1.call-start = ((), (), s32[]{:S(2)}) async-start(), calls=%async_computation.3 | async-start | bytes 5406720 | tf_op jit(solution)/shard_map/all_gather | solution.py:154
  489.8 72.3 %copy-start.4 = (f32[64,576]{0,1:T(8,128)}, f32[64,576]{0,1:T(8,128)S(1)}, u32[]{:S(2)}) copy-start(f32[64,576]{0,1:T(8,128)S(1)} %copy.300) | copy-start | bytes 442372
  490.6 206.1 %all-gather.19.cloned.1.call-start = ((), (), s32[]{:S(2)}) async-start(), calls=%async_computation.4 | async-start | bytes 5406720 | tf_op jit(solution)/shard_map/all_gather | solution.py:154
  632.2 72.3 %copy-start.6 = (f32[64,576]{0,1:T(8,128)}, f32[64,576]{0,1:T(8,128)S(1)}, u32[]{:S(2)}) copy-start(f32[64,576]{0,1:T(8,128)S(1)} %copy.308) | copy-start | bytes 442372
  633.1 206.0 %all-gather.21.cloned.1.call-start = ((), (), s32[]{:S(2)}) async-start(), calls=%async_computation.5 | async-start | bytes 5406720 | tf_op jit(solution)/shard_map/all_gather | solution.py:154
  774.6 72.3 %copy-start.8 = (f32[64,576]{0,1:T(8,128)}, f32[64,576]{0,1:T(8,128)S(1)}, u32[]{:S(2)}) copy-start(f32[64,576]{0,1:T(8,128)S(1)} %copy.316) | copy-start | bytes 442372
  775.4 206.6 %all-gather.23.cloned.1.call-start = ((), (), s32[]{:S(2)}) async-start(), calls=%async_computation.6 | async-start | bytes 5406720 | tf_op jit(solution)/shard_map/all_gather | solution.py:154
  853.3 65.2 %copy-start.21 = (f32[64,64]{1,0:T(8,128)S(1)}, f32[64,64]{1,0:T(8,128)}, u32[]{:S(2)}) copy-start(f32[64,64]{1,0:T(8,128)} %copy-done.20) | copy-start | bytes 49156
  853.3 65.8 %copy-start.1 = (f32[64,576]{0,1:T(8,128)S(1)}, f32[64,576]{0,1:T(8,128)}, u32[]{:S(2)}) copy-start(f32[64,576]{0,1:T(8,128)} %copy-done) | copy-start | bytes 442372
  878.1 41.8 %copy-start.13 = (f32[128,128]{1,0:T(8,128)S(1)}, f32[128,128]{1,0:T(8,128)}, u32[]{:S(2)}) copy-start(f32[128,128]{1,0:T(8,128)} %shard_map.59) | copy-start | bytes 196612
  878.1 42.5 %copy-start.3 = (f32[64,576]{0,1:T(8,128)S(1)}, f32[64,576]{0,1:T(8,128)}, u32[]{:S(2)}) copy-start(f32[64,576]{0,1:T(8,128)} %copy-done.2) | copy-start | bytes 442372
  878.1 44.0 %copy-start.14 = (f32[128,128]{1,0:T(8,128)S(1)}, f32[128,128]{1,0:T(8,128)}, u32[]{:S(2)}) copy-start(f32[128,128]{1,0:T(8,128)} %shard_map.60) | copy-start | bytes 196612
  878.1 44.0 %copy-start.5 = (f32[64,576]{0,1:T(8,128)S(1)}, f32[64,576]{0,1:T(8,128)}, u32[]{:S(2)}) copy-start(f32[64,576]{0,1:T(8,128)} %copy-done.4) | copy-start | bytes 442372
  878.1 45.4 %copy-start.15 = (f32[128,128]{1,0:T(8,128)S(1)}, f32[128,128]{1,0:T(8,128)}, u32[]{:S(2)}) copy-start(f32[128,128]{1,0:T(8,128)} %shard_map.61) | copy-start | bytes 196612
  878.1 45.4 %copy-start.7 = (f32[64,576]{0,1:T(8,128)S(1)}, f32[64,576]{0,1:T(8,128)}, u32[]{:S(2)}) copy-start(f32[64,576]{0,1:T(8,128)} %copy-done.6) | copy-start | bytes 442372
  878.2 46.8 %copy-start.16 = (f32[128,128]{1,0:T(8,128)S(1)}, f32[128,128]{1,0:T(8,128)}, u32[]{:S(2)}) copy-start(f32[128,128]{1,0:T(8,128)} %shard_map.62) | copy-start | bytes 196612
  878.2 46.8 %copy-start.9 = (f32[64,576]{0,1:T(8,128)S(1)}, f32[64,576]{0,1:T(8,128)}, u32[]{:S(2)}) copy-start(f32[64,576]{0,1:T(8,128)} %copy-done.8) | copy-start | bytes 442372
  899.4 26.9 %copy-start.17 = (f32[128,128]{1,0:T(8,128)S(1)}, f32[128,128]{1,0:T(8,128)}, u32[]{:S(2)}) copy-start(f32[128,128]{1,0:T(8,128)} %shard_map.63) | copy-start | bytes 196612
  917.6 72.3 %copy-start.10 = (f32[64,576]{0,1:T(8,128)}, f32[64,576]{0,1:T(8,128)S(1)}, u32[]{:S(2)}) copy-start(f32[64,576]{0,1:T(8,128)S(1)} %copy.324) | copy-start | bytes 442372
  1057.2 9.2 copy-start.22
Sparse Core Ops, SparseCore 0:
  34.4 85.3 all-reduce.1
Sparse Core Ops, SparseCore 1:
  77.2 69.4 all-gather.12
  348.3 63.2 all-gather.14
  490.7 63.5 all-gather.16
  633.2 63.5 all-gather.18
  775.5 63.5 all-gather.20
  918.5 63.5 all-gather.22
where the time goes:
time: 1090 us; the launch traced here: 1070 us
  waiting for transfers between devices  355 us (33%)
  local copies, waits for them, and re-layouts  263 us (24%)
  matrix products  183 us (17%)
  Pallas kernels  156 us (14%)
  other arithmetic  96.3 us (9%)
  between operations  16.9 us (2%)
    all_gather x6, waiting for transfers between devices, local(): lax.all_gather(current, ('tm', 'panel'), axis=0, tiled=True)  308 us
    dot_general x6, matrix products, local(): jnp.dot(covariance, lax.all_gather(current, ('tm', 'panel'), axis=0, tile...  148 us
    pallas_call x7, Pallas kernels, grams(): pl.pallas_call(lambda *refs: gram_kernel(sizes, *refs), out_shape=jax.Sha...  144 us
    rev x2, local copies, waits for them, and re-layouts, local(): jnp.transpose(blocks, (2, 1, 0))[:, :0:-1, :]  86.7 us
    unnamed x92, local copies, waits for them, and re-layouts  79.9 us
    all_gather x6, local copies, waits for them, and re-layouts, local(): lax.all_gather(current, ('tm', 'panel'), axis=0, tiled=True)  47.2 us
    psum x1, waiting for transfers between devices, local(): summed = lax.psum(lag_products(series, extended), 'tm')  41.9 us
    another operation x18, other arithmetic, local(): factor = jnp.linalg.cholesky(gram_matrix)  39.2 us
  transfers between devices with their start and end apart: 9, of which 8 were waited for; matrix products, arithmetic and copies ran while one was open for 16% of the time, Pallas kernels for 2%

commit v1 on v0

v1 whole, which is shorter than its diff:
```python
import jax
import jax.numpy as jnp
from jax import lax
from jax.experimental import pallas as pl
from jax.experimental.pallas import tpu as pltpu
from jax.sharding import PartitionSpec as P

M = 384
ITERS = 6
MESH = pl.DeviceIdType.MESH
EXACT = lax.Precision.HIGHEST
F32 = jnp.float32
BF16 = jnp.bfloat16
VMEM = pl.BlockSpec(memory_space=pltpu.VMEM)


def flip(index, mask):
    bit = 1
    while bit <= mask:
        if mask & bit:
            index = index + bit - 2 * bit * ((index // bit) % 2)
        bit *= 2
    return index


def round_up(value, unit):
    return -(-value // unit) * unit


class Plan:
    def __init__(self, channels, days, width, tm_size, panel_size):
        self.channels = channels
        self.days = days
        self.width = width
        self.tm_size = tm_size
        self.panel_size = panel_size
        self.lags = M // (tm_size * panel_size)
        self.phases = max(r for r in (1, 2, 3, 4) if self.lags % r == 0)
        self.groups = 8 if (8 * self.phases) % 16 == 0 else 16
        self.run = self.lags * panel_size
        self.pad = round_up(self.run + self.lags, self.groups * self.phases)
        self.reach = M + self.pad
        self.units = self.reach // self.phases
        self.steps = self.units // self.groups
        self.depth = days + 128
        self.heads = self.lags // self.phases
        self.rows = self.heads * channels
        self.lanes = 128 * ((self.phases * width + 127) // 128)
        self.columns = tm_size // 2


def series_kernel(size, s_ref, o_ref, held, send_sem, recv_sem):
    me = lax.axis_index("tm")
    days = s_ref.shape[1]
    barrier = pltpu.get_barrier_semaphore()
    for distance in range(1, size):
        pl.semaphore_signal(
            barrier, inc=1, device_id={"tm": (me + distance) % size}, device_id_type=MESH
        )
    pl.semaphore_wait(barrier, size - 1)
    copies = []
    for distance in range(1, size):
        copy = pltpu.make_async_remote_copy(
            src_ref=s_ref,
            dst_ref=held.at[distance],
            send_sem=send_sem.at[distance],
            recv_sem=recv_sem.at[distance],
            device_id={"tm": (me + distance) % size},
            device_id_type=MESH,
        )
        copy.start()
        copies.append(copy)
    o_ref[me] = s_ref[...]
    for distance, copy in enumerate(copies, 1):
        copy.wait_recv()
        o_ref[(me + size - distance) % size] = held[distance]
    for copy in copies:
        copy.wait_send()


def all_days(series, size):
    return pl.pallas_call(
        lambda *refs: series_kernel(size, *refs),
        out_shape=jax.ShapeDtypeStruct((size,) + series.shape, F32),
        in_specs=[VMEM],
        out_specs=VMEM,
        scratch_shapes=[
            pltpu.VMEM((size,) + series.shape, F32),
            pltpu.SemaphoreType.DMA((size,)),
            pltpu.SemaphoreType.DMA((size,)),
        ],
        compiler_params=pltpu.CompilerParams(collective_id=0, has_side_effects=True),
    )(series)


def covariance_kernel(plan, xh_ref, xl_ref, gh_ref, gl_ref, n_ref, near_ref, c_ref, wide, sem):
    channels, phases = plan.channels, plan.phases
    unit = plan.groups * channels
    together = max(g for g in (1, 2) if plan.steps % g == 0 and g * unit <= 768)

    def product(step, carry):
        pieces_h, pieces_l = [], []
        for g in range(together):
            start = pl.multiple_of((step * together + g) * plan.groups * phases, 16)
            pieces_h.append(gh_ref[pl.ds(start, plan.depth), :])
            pieces_l.append(gl_ref[pl.ds(start, plan.depth), :])
        high = jnp.concatenate(pieces_h, axis=1) if together > 1 else pieces_h[0]
        low = jnp.concatenate(pieces_l, axis=1) if together > 1 else pieces_l[0]
        total = jnp.dot(xh_ref[...], high, preferred_element_type=F32)
        total += jnp.dot(xh_ref[...], low, preferred_element_type=F32)
        total += jnp.dot(xl_ref[...], high, preferred_element_type=F32)
        at = pl.ds(pl.multiple_of(step * together * unit, 128), together * unit)
        counts = n_ref[:, at]
        for p in range(phases):
            rows = slice(p * channels, (p + 1) * channels)
            near_ref[rows, at] = total[rows] / counts[p : p + 1]
        return carry

    lax.fori_loop(0, plan.steps // together, product, 0)

    def weave(step, carry):
        block = near_ref[:, pl.ds(pl.multiple_of(step * unit, 128), unit)]
        pieces = [
            block[p * channels : (p + 1) * channels, g * channels : (g + 1) * channels]
            for g in range(plan.groups)
            for p in range(phases)
        ]
        at = pl.ds(pl.multiple_of(step * unit * phases, 128), unit * phases)
        wide[0, :, at] = jnp.concatenate(pieces, axis=1)
        return carry

    lax.fori_loop(0, plan.steps, weave, 0)

    total = plan.reach * channels
    core = lax.axis_index("tm") % 2
    jump = plan.run * channels
    if jump % 128:

        def choose(group, carry):
            rows = pl.ds(pl.multiple_of(group * 8, 8), 8)
            whole = wide[0, rows, :]
            back = pltpu.roll(whole, jump, 1)
            wide[0, rows, :] = jnp.where(core == 1, back, whole)
            return carry

        lax.fori_loop(0, channels // 8, choose, 0)
    slots = {}
    order = []
    for i in range(plan.lags):
        shift = ((plan.pad - i) * channels) % 128
        if shift not in slots:
            slots[shift] = len(slots)
    slots = {s: n for n, s in enumerate(sorted(slots))}
    copies = []
    for shift, slot in slots.items():
        if slot > 0:

            def turn(group, carry):
                rows = pl.ds(pl.multiple_of(group * 8, 8), 8)
                wide[slot, rows, :] = pltpu.roll(wide[0, rows, :], total - shift, 1)
                return carry

            lax.fori_loop(0, channels // 8, turn, 0)
        for i in range(plan.lags):
            first = (plan.pad - i) * channels
            if first % 128 != shift:
                continue
            start = first - shift
            if jump % 128 == 0:
                start = pl.multiple_of(start - jump * core, 128)
            copy = pltpu.make_async_copy(
                wide.at[slot, :, pl.ds(start, M * channels)],
                c_ref.at[pl.ds(i * channels, channels), :],
                sem.at[i],
            )
            copy.start()
            copies.append(copy)
    for copy in copies:
        copy.wait()


def split(array):
    high = lax.reduce_precision(array, 8, 7)
    return high.astype(BF16), (array - high).astype(BF16)


def covariance_rows(plan, days_by_device):
    channels, phases, days = plan.channels, plan.phases, plan.days
    size = plan.tm_size
    whole = jnp.transpose(days_by_device, (1, 0, 2)).reshape(channels, days)
    turned = jnp.transpose(days_by_device, (0, 2, 1)).reshape(days, channels)
    tm, panel = lax.axis_index("tm"), lax.axis_index("panel")
    base = -(tm // 2) * 2 * plan.run - panel * plan.lags - plan.pad
    stretch = plan.depth + plan.groups * phases * (plan.steps - 1)
    padded = jnp.pad(turned, ((M + plan.pad, plan.depth - days + M + plan.pad), (0, 0)))
    length = stretch + phases * (plan.groups - 1)
    near_days = lax.dynamic_slice(padded, (M + plan.pad + base, jnp.int32(0)), (length, channels))
    gathered = jnp.concatenate(
        [near_days[phases * g : phases * g + stretch] for g in range(plan.groups)], axis=1
    )
    shifted = jnp.concatenate(
        [jnp.pad(whole, ((0, 0), (p, plan.depth - days - p))) for p in range(phases)], axis=0
    )
    lag = base + jnp.arange(plan.units * channels) // channels * phases
    lag = lag[None, :] + jnp.arange(phases)[:, None]
    counts = (days - jnp.abs(lag)).astype(F32)
    shifts = len({((plan.pad - i) * channels) % 128 for i in range(plan.lags)} | {0})
    return pl.pallas_call(
        lambda *refs: covariance_kernel(plan, *refs),
        out_shape=(
            jax.ShapeDtypeStruct((phases * channels, plan.units * channels), F32),
            jax.ShapeDtypeStruct((plan.lags * channels, M * channels), F32),
        ),
        in_specs=[VMEM] * 5,
        out_specs=(VMEM, pl.BlockSpec(memory_space=pl.ANY)),
        scratch_shapes=[
            pltpu.VMEM((shifts, channels, plan.reach * channels), F32),
            pltpu.SemaphoreType.DMA((plan.lags,)),
        ],
        compiler_params=pltpu.CompilerParams(vmem_limit_bytes=60 * 1024 * 1024),
    )(*split(shifted), *split(gathered), counts)


def factor_and_inverse(gram, width):
    lanes = 2 * width
    row = lax.broadcasted_iota(jnp.int32, (width, lanes), 0)
    lane = lax.broadcasted_iota(jnp.int32, (width, lanes), 1)
    work = jnp.where(lane < width, gram, jnp.where(lane - width == row, 1.0, 0.0))
    for j in range(width):
        pivot_row = work[j : j + 1, :]
        scale = lax.rsqrt(jnp.broadcast_to(pivot_row[:, j : j + 1], (1, lanes)))
        pivot_row = pivot_row * scale
        column = jnp.broadcast_to(work[:, j : j + 1], (width, lanes)) * scale
        work = jnp.where(row > j, work - column * pivot_row, jnp.where(row == j, pivot_row, work))
    return jnp.where((lane < width) & (lane < row), 0.0, work)


def lanczos_kernel(
    plan,
    near_ref,
    x_ref,
    basis_ref,
    diag_ref,
    off_ref,
    lh,
    ll,
    zg,
    zh,
    zl,
    parts,
    q_s,
    z_s,
    v_s,
    guess,
    y_send,
    y_recv,
    g_held,
    g_got,
    p_send,
    p_recv,
    c_send,
    c_recv,
    g_send,
    g_recv,
    y_sems,
):
    channels, phases, width = plan.channels, plan.phases, plan.width
    heads, rows, lanes = plan.heads, plan.rows, plan.lanes
    panel_size, columns = plan.panel_size, plan.columns
    tm, panel = lax.axis_index("tm"), lax.axis_index("panel")
    core, k = tm % 2, tm // 2
    bits = columns.bit_length() - 1

    partners = [("tm", flip(tm, 1 << b)) for b in range(bits + 1)]
    partners += [("panel", flip(panel, d)) for d in range(1, panel_size)]
    barrier = pltpu.get_barrier_semaphore()
    for axis, other in partners:
        pl.semaphore_signal(barrier, inc=1, device_id={axis: other}, device_id_type=MESH)
    gram_partners = [("tm", flip(tm, 1 << b)) for b in range(bits + 1)]
    gram_partners += [
        ("panel", flip(panel, 1 << b)) for b in range(panel_size.bit_length() - 1)
    ]

    zero = jnp.zeros((rows, lanes), F32)
    q_s[...] = zero
    v_s[...] = zero
    z_s[...] = x_ref[...]
    guess[...] = jnp.zeros_like(guess)
    zg[0, k, panel] = x_ref[...]
    pl.semaphore_wait(barrier, len(partners))

    lane1 = lax.broadcasted_iota(jnp.int32, (width, 2 * width), 1)

    def spread(pair):
        low = jnp.where(lane1 < width, pair, 0.0)
        high = pltpu.roll(low, width, 1)
        none = jnp.zeros_like(low)
        out = []
        for p in range(lanes // width):
            here = low if p % 2 == 0 else high
            if p >= phases:
                here = none
            line = [here if t == p // 2 else none for t in range(lanes // (2 * width))]
            out.append(jnp.concatenate(line, axis=1) if len(line) > 1 else line[0])
        return jnp.concatenate(out, axis=0)

    def folded(square):
        even = odd = None
        for p in range(phases):
            block = square[p * width : (p + 1) * width, (p // 2) * 2 * width :][:, : 2 * width]
            if p % 2 == 0:
                even = block if even is None else even + block
            else:
                odd = block if odd is None else odd + block
        if odd is not None:
            even = even + pltpu.roll(odd, width, 1)
        return even

    def times(a, b):
        return jnp.dot(a, b, precision=EXACT, preferred_element_type=F32)

    def times_t(a, b):
        return lax.dot_general(
            a, b, (((1,), (1,)), ((), ())), precision=EXACT, preferred_element_type=F32
        )

    def t_times(a, b):
        return lax.dot_general(
            a, b, (((0,), (0,)), ((), ())), precision=EXACT, preferred_element_type=F32
        )

    def remote(src, dst, send, recv, axis, other):
        return pltpu.make_async_remote_copy(
            src_ref=src,
            dst_ref=dst,
            send_sem=send,
            recv_sem=recv,
            device_id={axis: other},
            device_id_type=MESH,
        )

    def panel_copy(par, d):
        slot = zg.at[par, k, panel]
        return remote(slot, slot, p_send.at[par, d], p_recv.at[par, d], "panel", flip(panel, d))

    def panel_arrival(par, d):
        slot = zg.at[par, k, flip(panel, d)]
        return remote(slot, slot, p_send.at[par, d], p_recv.at[par, d], "panel", flip(panel, d))

    orders = {}
    for d in range(panel_size):
        order = list(range(bits))
        orders[d] = order if d < panel_size // 2 else order[::-1]

    def column_copy(par, mask, d, bit):
        slot = zg.at[par, flip(k, mask), flip(panel, d)]
        n = (mask ^ (1 << bit)) * panel_size + d
        return remote(
            slot, slot, c_send.at[par, n], c_recv.at[par, n], "tm", flip(tm, 2 << bit)
        )

    def column_arrival(par, mask, d):
        order = orders[d]
        bit = [b for b in order if mask & (1 << b)][-1]
        slot = zg.at[par, flip(k, mask), flip(panel, d)]
        n = mask * panel_size + d
        return remote(
            slot, slot, c_send.at[par, n], c_recv.at[par, n], "tm", flip(tm, 2 << bit)
        )

    def last_stage(mask, d):
        return max([s for s, b in enumerate(orders[d]) if mask & (1 << b)], default=-1)

    def gram_copy(par, s):
        axis, other = gram_partners[s]
        return remote(
            g_held.at[par, s], g_got.at[par, s], g_send.at[par, s], g_recv.at[par, s], axis, other
        )

    def local_gram(par):
        q, z = q_s[...], z_s[...]
        first = folded(t_times(q, z))
        second = folded(t_times(z, z))
        g_held[par, 0] = jnp.where(lane1 < width, first, pltpu.roll(second, width, 1))
        gram_copy(par, 0).start()

    def gram_stage(par, s):
        copy = gram_copy(par, s)
        copy.wait_recv()
        g_held[par, s + 1] = g_held[par, s] + g_got[par, s]
        copy.wait_send()
        if s + 1 < len(gram_partners):
            gram_copy(par, s + 1).start()

    def small(par, j):
        both = g_held[par, len(gram_partners)]
        rest = jnp.where(lane1 < width, both, 0.0)
        square = t_times(rest, rest)[:width]
        gram = pltpu.roll(both, width, 1) - square
        work = factor_and_inverse(gram, width)
        diag = rest + guess[...]
        diag_ref[j] = diag[:, :width]
        off_ref[j] = work[:, :width]
        spread_rest = spread(rest)
        spread_r = spread(work)
        spread_l = spread(pltpu.roll(work, width, 1))
        q = q_s[...]
        after = z_s[...] - times(q, spread_rest)
        following = times_t(after, spread_l)
        for p in range(phases):
            block = following[:, (p // 2) * 2 * width :][:, : 2 * width]
            if p % 2:
                block = pltpu.roll(block, width, 1)
            for h in range(heads):
                basis_ref[j, pl.ds((h * phases + p) * channels, channels), :] = block[
                    h * channels : (h + 1) * channels, :width
                ]
        return diag, spread_rest, spread_r, spread_l, following

    def build(own):
        total = plan.units * channels
        back = plan.run // phases * channels
        stride = 2 * back
        for p in range(phases):

            def chunk(c, carry):
                at = pl.multiple_of(p * channels + c * 16, 16)
                part = near_ref[pl.ds(at, 16), :]
                if not own:
                    part = jnp.where(
                        core == 1, pltpu.roll(part, total - back, 1), pltpu.roll(part, back, 1)
                    )
                for i in range(1 - phases, plan.lags):
                    if (plan.pad - i - p) % phases:
                        continue
                    u0 = (plan.pad - i - p) // phases
                    turned = pltpu.roll(part, total - u0 * channels, 1)
                    pieces = [turned[:, n * stride : n * stride + back] for n in range(columns)]
                    line = jnp.concatenate(pieces, axis=1)
                    high = line.astype(BF16)
                    low = (line - high.astype(F32)).astype(BF16)
                    to = pl.ds(pl.multiple_of((i + phases - 1) * channels + c * 16, 16), 16)
                    lh[int(own), to, :] = high
                    ll[int(own), to, :] = low
                return carry

            lax.fori_loop(0, channels // 16, chunk, 0)

    def product(which):
        high, low = zh[...], zl[...]
        parts[...] = jnp.dot(lh[which], high, preferred_element_type=F32)
        parts[...] += jnp.dot(lh[which], low, preferred_element_type=F32)
        parts[...] += jnp.dot(ll[which], high, preferred_element_type=F32)
        lane = lax.broadcasted_iota(jnp.int32, (channels, lanes), 1)
        out = []
        for h in range(heads):
            total = None
            for delta in range(1 - phases, phases):
                i = h * phases + delta + phases - 1
                term = parts[i * channels : (i + 1) * channels, :]
                if delta:
                    term = pltpu.roll(term, (delta * width) % lanes, 1)
                    if delta > 0:
                        keep = lane >= delta * width
                    else:
                        keep = lane < (phases + delta) * width
                    term = jnp.where(keep, term, 0.0)
                total = term if total is None else total + term
            out.append(total)
        whole = jnp.concatenate(out, axis=0) if heads > 1 else out[0]
        if phases * width < lanes:
            whole = jnp.where(
                lax.broadcasted_iota(jnp.int32, whole.shape, 1) < phases * width, whole, 0.0
            )
        return whole

    def iteration(j, carry):
        par = j % 2
        sends = []
        for d in range(1, panel_size):
            copy = panel_copy(par, d)
            copy.start()
            sends.append(copy)
        for bit in orders[0]:
            copy = column_copy(par, 0, 0, bit)
            copy.start()
            sends.append(copy)
        local_gram(par)
        stages = list(range(len(gram_partners)))

        def next_stage():
            if stages:
                gram_stage(par, stages.pop(0))

        for d in range(1, panel_size):
            panel_arrival(par, d).wait_recv()
            for bit in orders[d]:
                copy = column_copy(par, 0, d, bit)
                copy.start()
                sends.append(copy)
            next_stage()
        waited = set()
        for s in range(bits - 1):
            for d in range(panel_size):
                for mask in range(1, columns):
                    if last_stage(mask, d) != s:
                        continue
                    column_arrival(par, mask, d).wait_recv()
                    waited.add((mask, d))
                    for bit in orders[d][s + 1 :]:
                        copy = column_copy(par, mask, d, bit)
                        copy.start()
                        sends.append(copy)
                    next_stage()
        while stages:
            next_stage()
        diag, spread_rest, spread_r, spread_l, following = small(par, j)
        v_part = times(v_s[...], spread_rest)
        q_r = times_t(q_s[...], spread_r) + times(following, spread(diag))
        guess[...] = diag

        @pl.when(j == 0)
        def _():
            build(False)
            build(True)

        for mask in range(1, columns):
            for d in range(panel_size):
                if (mask, d) not in waited:
                    column_arrival(par, mask, d).wait_recv()
        for n in range(columns):
            for d in range(panel_size):
                block = zg[par, n, d]
                high = block.astype(BF16)
                at = pl.ds((n * panel_size + d) * rows, rows)
                zh[at, :] = high
                zl[at, :] = (block - high.astype(F32)).astype(BF16)
        y_send[par] = product(0)
        to_other = remote(
            y_send.at[par], y_recv.at[par], y_sems.at[par, 0], y_sems.at[par, 1], "tm", flip(tm, 1)
        )
        to_other.start()
        mine = product(1)
        to_other.wait_recv()
        y = mine + y_recv[par]
        v = times_t(y - v_part, spread_l)
        z = v - q_r
        v_s[...] = v
        z_s[...] = z
        q_s[...] = following
        zg[1 - par, k, panel] = z
        for copy in sends:
            copy.wait_send()
        to_other.wait_send()
        return carry

    lax.fori_loop(0, ITERS, iteration, 0)
    par = ITERS % 2
    local_gram(par)
    for s in range(len(gram_partners)):
        gram_stage(par, s)
    small(par, ITERS)


def lanczos(plan, near, packed):
    channels, phases, width = plan.channels, plan.phases, plan.width
    rows, lanes = plan.rows, plan.lanes
    blocks = plan.columns * plan.panel_size
    groups = (plan.lags + phases - 1) * channels
    stages = (plan.tm_size * plan.panel_size).bit_length() - 1
    block = (rows, lanes)
    pair = (width, 2 * width)
    dma = pltpu.SemaphoreType.DMA
    return pl.pallas_call(
        lambda *refs: lanczos_kernel(plan, *refs),
        out_shape=(
            jax.ShapeDtypeStruct((ITERS + 1, plan.lags * channels, width), F32),
            jax.ShapeDtypeStruct((ITERS + 1, width, width), F32),
            jax.ShapeDtypeStruct((ITERS + 1, width, width), F32),
        ),
        in_specs=[VMEM] * 2,
        out_specs=(VMEM,) * 3,
        scratch_shapes=[
            pltpu.VMEM((2, groups, blocks * rows), BF16),
            pltpu.VMEM((2, groups, blocks * rows), BF16),
            pltpu.VMEM((2, plan.columns, plan.panel_size) + block, F32),
            pltpu.VMEM((blocks * rows, lanes), BF16),
            pltpu.VMEM((blocks * rows, lanes), BF16),
            pltpu.VMEM((groups, lanes), F32),
            pltpu.VMEM(block, F32),
            pltpu.VMEM(block, F32),
            pltpu.VMEM(block, F32),
            pltpu.VMEM(pair, F32),
            pltpu.VMEM((2,) + block, F32),
            pltpu.VMEM((2,) + block, F32),
            pltpu.VMEM((2, stages + 1) + pair, F32),
            pltpu.VMEM((2, stages) + pair, F32),
            dma((2, plan.panel_size)),
            dma((2, plan.panel_size)),
            dma((2, blocks)),
            dma((2, blocks * max(1, plan.columns.bit_length()))),
            dma((2, stages)),
            dma((2, stages)),
            dma((2, 2)),
        ],
        compiler_params=pltpu.CompilerParams(
            collective_id=1, has_side_effects=True, vmem_limit_bytes=60 * 1024 * 1024
        ),
    )(near, packed)


def local(series, start_block):
    channels, day_count = series.shape
    tm_size = lax.axis_size("tm")
    panel_size = lax.axis_size("panel")
    width = start_block.shape[1]
    plan = Plan(channels, day_count * tm_size, width, tm_size, panel_size)
    near, covariance = covariance_rows(plan, all_days(series, tm_size))
    packed = start_block.reshape(plan.heads, plan.phases, channels, width)
    packed = jnp.transpose(packed, (0, 2, 1, 3)).reshape(plan.rows, plan.phases * width)
    packed = jnp.pad(packed, ((0, 0), (0, plan.lanes - plan.phases * width)))
    basis, diag, off = lanczos(plan, near, packed)
    return covariance, basis, diag[1:], off


def solution(mesh):
    placed = (P(None, "tm"), P(("tm", "panel"), None))
    return jax.shard_map(
        local,
        mesh=mesh,
        in_specs=placed,
        out_specs=(P(("tm", "panel"), None), P(None, ("tm", "panel"), None), P(), P()),
        check_vma=False,
    )
```

time: 1090 us -> 365 us (0.33); the launches traced: 1070 us -> 364 us
  waiting for transfers between devices: 355 us -> 0 us
  local copies, waits for them, and re-layouts: 263 us -> 25.6 us
  matrix products: 183 us -> 0 us
  Pallas kernels: 156 us -> 331 us
  other arithmetic: 96.3 us -> 6.94 us
  between operations: 16.9 us -> 0.73 us
    all_gather x6 -> x0, waiting for transfers between devices: 308 us -> none  [local(): lax.all_gather(current, ('tm', 'panel'), axis=0, tiled=True)]
    dot_general x35 -> x0, matrix products: 179 us -> none  [the longest x6 148 us: local(): jnp.dot(covariance, lax.all_gather(current, ('tm', 'panel'), axis=0, tile...]
    pallas_call x8 -> x3, Pallas kernels: 156 us -> 331 us  [the longest x1 282 us: lanczos(): pl.pallas_call(lambda *refs: lanczos_kernel(plan, *refs), out_shape=(jax....]
    rev x2 -> x0, local copies, waits for them, and re-layouts: 86.7 us -> none  [local(): jnp.transpose(blocks, (2, 1, 0))[:, :0:-1, :]]
    another operation x36 -> x0, other arithmetic: 85.2 us -> none  [the longest x18 39.2 us: local(): factor = jnp.linalg.cholesky(gram_matrix)]
    unnamed x92 -> x11, local copies, waits for them, and re-layouts: 79.9 us -> 3.75 us
    all_gather x6 -> x0, local copies, waits for them, and re-layouts: 47.2 us -> none  [local(): lax.all_gather(current, ('tm', 'panel'), axis=0, tiled=True)]
    psum x1 -> x0, waiting for transfers between devices: 41.9 us -> none  [local(): summed = lax.psum(lag_products(series, extended), 'tm')]
  transfers between devices with their start and end apart: 9 -> 0, of which waited for: 8 -> 0; matrix products, arithmetic and copies ran while one was open for 16% -> 0% of each run, Pallas kernels for 2% -> 0%
where the time goes in v1:
time: 365 us; the launch traced here: 364 us
  Pallas kernels  331 us (91%)
  local copies, waits for them, and re-layouts  25.6 us (7%)
  other arithmetic  6.94 us (2%)
    pallas_call x1, Pallas kernels, lanczos(): pl.pallas_call(lambda *refs: lanczos_kernel(plan, *refs), out_shape=(jax....  282 us
    pallas_call x1, Pallas kernels, covariance_rows(): pl.pallas_call(lambda *refs: covariance_kernel(plan, *refs), out_shape=(j...  38.3 us
    pallas_call x1, Pallas kernels, all_days(): pl.pallas_call(lambda *refs: series_kernel(size, *refs), out_shape=jax.Sh...  10.9 us
    concatenate x1, local copies, waits for them, and re-layouts, covariance_rows(): jnp.concatenate([near_days[phases * g:phases * g + stretch] for g in rang...  9.16 us
    slice x1, local copies, waits for them, and re-layouts, covariance_rows(): near_days[phases * g:phases * g + stretch]  8.69 us

profile of v1, /device:TPU:0, one launch (start us, length us, event | category | flops | bytes accessed | tf_op | source)
XLA Modules:
  0.0 364.4 jit_solution(3070585461096594763)
XLA Ops:
  0.7 10.9 %shard_map.57 = f32[8,48,256]{2,1,0:T(8,128)} custom-call(f32[48,256]{1,0:T(8,128)} %refs_0_.1), custom_call_target="tpu_custom_call" | custom-call | tf_op jit(solution)/shard_map/pallas_call | solution.py:82
  11.6 2.3 copy.11
  13.9 8.7 %pad_dynamic-slice_fusion.7 = (f32[2592,48]{1,0:T(8,128)S(1)}, f32[2592,48]{1,0:T(8,128)S(1)}, f32[2592,48]{1,0:T(8,128)}, f32[2592,48]{1,0:T(8,128)}, f32[2592,...) fusion(s32[]{:T(128)S(6)} %add.61, f32[2048,48]{1,0:T(8,128)} %bitcast.8, ...), kind=kLoop, calls=%fused_computation.10 | loop fusion | bytes 4374560 | tf_op jit(solution)/shard_map/slice | solution.py:199
  22.6 9.2 %concatenate.7 = f32[2592,384]{1,0:T(8,128)} concatenate(f32[2592,48]{1,0:T(8,128)S(1)} %get-tuple-element.25, f32[2592,48]{1,0:T(8,128)} %get-tuple-element.26, f32[2592,48]{1,0:T(8,128)} %get-tuple-element.27, f32[2592,48]{1,0:T(8,128)} %get-tuple-element.28, f32[2592,48]{1,0:T(8,128)} %get-tuple-element.29, f32[2592,48]{1,0:T(8,128)} %get-tuple-element.30, ...), dimensions={1} | concatenate | bytes 7962624 | tf_op jit(solution)/shard_map/concatenate | solution.py:198
  31.8 0.0 copy-start
  31.8 4.7 %fusion = (bf16[2592,384]{1,0:T(8,128)(2,1)}, bf16[2592,384]{1,0:T(8,128)(2,1)}) fusion(f32[2592,384]{1,0:T(8,128)} %concatenate.7), kind=kLoop, calls=%fused_computation.2 | loop fusion | flops 3981312 | bytes 7962624 | tf_op jit(solution)/shard_map/convert_element_type | solution.py:184
  36.4 0.7 subtract_convert_fusion.refs_4_
  37.1 0.0 copy-done
  37.2 1.6 fusion.1
  38.7 0.0 copy-start.3
  38.7 38.3 %shard_map.58 = (f32[192,5376]{1,0:T(8,128)}, f32[576,18432]{1,0:T(8,128)}) custom-call(bf16[192,2176]{1,0:T(8,128)(2,1)} %get-tuple-element.33.refs_0_, bf16[192,2176]{1,0:T(8,128)(2,1)} %get-tuple-element.32.refs_1_, bf16[2592,384]{1,0:T(8,128)(2,1)} %get-tuple-element.23.refs_2_, bf16[2592,384]{1,0:T(8,128)(2,1)} %get-tuple-element.22.refs_3_, ...), custom_call_target="tpu_custom_call" | custom-call | tf_op jit(solution)/shard_map/pallas_call | solution.py:208
  77.1 0.0 copy-done.3
  77.1 0.1 copy.12
  77.2 0.1 copy.13
  77.3 0.9 reshape.38.refs_1_
  78.2 281.9 %shard_map.59 = (f32[7,576,64]{2,1,0:T(8,128)}, f32[7,64,64]{2,1,0:T(8,128)}, f32[7,64,64]{2,1,0:T(8,128)}) custom-call(f32[192,5376]{1,0:T(8,128)} %get-tuple-element.10.refs_0_, f32[144,256]{1,0:T(8,128)} %reshape.38.refs_1_), custom_call_target="tpu_custom_call" | custom-call | tf_op jit(solution)/shard_map/pallas_call | solution.py:574
  360.1 0.0 copy-start.2
  360.1 0.0 copy-start.1
  360.1 2.9 copy.14
  363.0 0.0 copy-done.2
  363.0 0.7 slice.35
  363.7 0.0 copy-done.1
  363.7 0.7 copy.17
  (2 shorter events, 0.0 us)
Async XLA Ops:
  31.8 5.4 %copy-start = (f32[8,48,256]{2,1,0:T(8,128)S(1)}, f32[8,48,256]{2,1,0:T(8,128)}, u32[]{:S(2)}) copy-start(f32[8,48,256]{2,1,0:T(8,128)} %shard_map.57) | copy-start | bytes 1179652
  38.7 38.3 %copy-start.3 = (f32[576,64]{0,1:T(8,128)S(1)}, f32[576,64]{0,1:T(8,128)}, u32[]{:S(2)}) copy-start(f32[576,64]{0,1:T(8,128)} %param.3) | copy-start | bytes 442372
  360.1 2.9 copy-start.2
  360.1 3.6 copy-start.1

commit v2 on v1

--- a/solution.py
+++ b/solution.py
@@ -38,8 +38,9 @@
         self.phases = max(r for r in (1, 2, 3, 4) if self.lags % r == 0)
         self.groups = 8 if (8 * self.phases) % 16 == 0 else 16
         self.run = self.lags * panel_size
-        self.pad = round_up(self.run + self.lags, self.groups * self.phases)
-        self.reach = M + self.pad
+        self.pad = round_up(self.run + 2 * self.lags, self.groups * self.phases)
+        self.reach = round_up(M + self.pad + self.lags, (16 // self.groups) * 32)
+        self.reach = round_up(self.reach, self.groups * self.phases)
         self.units = self.reach // self.phases
         self.steps = self.units // self.groups
         self.depth = days + 128
@@ -47,6 +48,10 @@
         self.rows = self.heads * channels
         self.lanes = 128 * ((self.phases * width + 127) // 128)
         self.columns = tm_size // 2
+        self.halves = panel_size // 2
+
+    def offset(self, tm, panel):
+        return (tm // 2) * 2 * self.run + panel * self.lags + self.pad
 
 
 def series_kernel(size, s_ref, o_ref, held, send_sem, recv_sem):
@@ -93,9 +98,37 @@
     )(series)
 
 
-def covariance_kernel(plan, xh_ref, xl_ref, gh_ref, gl_ref, n_ref, near_ref, c_ref, wide, sem):
+def covariance_kernel(
+    plan, d_ref, n_ref, near_ref, c_ref, xh_ref, xl_ref, gh_ref, gl_ref, moved, wide, sem
+):
     channels, phases = plan.channels, plan.phases
     unit = plan.groups * channels
+    tm, panel = lax.axis_index("tm"), lax.axis_index("panel")
+    length = moved.shape[1]
+    for n in range(d_ref.shape[0]):
+        moved[:, n * d_ref.shape[2] : (n + 1) * d_ref.shape[2]] = d_ref[n]
+    moved[:, plan.days :] = jnp.zeros((channels, length - plan.days), F32)
+    for p in range(phases):
+        rows = slice(p * channels, (p + 1) * channels)
+        shifted = moved[:, : plan.depth]
+        if p:
+            shifted = pltpu.roll(shifted, p, 1)
+        high = shifted.astype(BF16)
+        xh_ref[rows, :] = high
+        xl_ref[rows, :] = (shifted - high.astype(F32)).astype(BF16)
+    moved[...] = pltpu.roll(moved[...], plan.offset(tm, panel), 1)
+
+    def transpose(step, carry):
+        at = pl.multiple_of(step * 128, 128)
+        window = moved[:, pl.ds(at, 256)]
+        stack = [window[:, phases * g : phases * g + 128] for g in range(plan.groups)]
+        block = jnp.concatenate(stack, axis=0).T
+        high = block.astype(BF16)
+        gh_ref[pl.ds(at, 128), :] = high
+        gl_ref[pl.ds(at, 128), :] = (block - high.astype(F32)).astype(BF16)
+        return carry
+
+    lax.fori_loop(0, gh_ref.shape[0] // 128, transpose, 0)
     together = max(g for g in (1, 2) if plan.steps % g == 0 and g * unit <= 768)
 
     def product(step, carry):
@@ -179,28 +212,10 @@
         copy.wait()
 
 
-def split(array):
-    high = lax.reduce_precision(array, 8, 7)
-    return high.astype(BF16), (array - high).astype(BF16)
-
-
 def covariance_rows(plan, days_by_device):
     channels, phases, days = plan.channels, plan.phases, plan.days
-    size = plan.tm_size
-    whole = jnp.transpose(days_by_device, (1, 0, 2)).reshape(channels, days)
-    turned = jnp.transpose(days_by_device, (0, 2, 1)).reshape(days, channels)
-    tm, panel = lax.axis_index("tm"), lax.axis_index("panel")
-    base = -(tm // 2) * 2 * plan.run - panel * plan.lags - plan.pad
-    stretch = plan.depth + plan.groups * phases * (plan.steps - 1)
-    padded = jnp.pad(turned, ((M + plan.pad, plan.depth - days + M + plan.pad), (0, 0)))
-    length = stretch + phases * (plan.groups - 1)
-    near_days = lax.dynamic_slice(padded, (M + plan.pad + base, jnp.int32(0)), (length, channels))
-    gathered = jnp.concatenate(
-        [near_days[phases * g : phases * g + stretch] for g in range(plan.groups)], axis=1
-    )
-    shifted = jnp.concatenate(
-        [jnp.pad(whole, ((0, 0), (p, plan.depth - days - p))) for p in range(phases)], axis=0
-    )
+    base = -plan.offset(lax.axis_index("tm"), lax.axis_index("panel"))
+    stretch = round_up(plan.depth + plan.groups * phases * (plan.steps - 1), 128)
     lag = base + jnp.arange(plan.units * channels) // channels * phases
     lag = lag[None, :] + jnp.arange(phases)[:, None]
     counts = (days - jnp.abs(lag)).astype(F32)
@@ -211,14 +226,19 @@
             jax.ShapeDtypeStruct((phases * channels, plan.units * channels), F32),
             jax.ShapeDtypeStruct((plan.lags * channels, M * channels), F32),
         ),
-        in_specs=[VMEM] * 5,
+        in_specs=[VMEM] * 2,
         out_specs=(VMEM, pl.BlockSpec(memory_space=pl.ANY)),
         scratch_shapes=[
+            pltpu.VMEM((phases * channels, plan.depth), BF16),
+            pltpu.VMEM((phases * channels, plan.depth), BF16),
+            pltpu.VMEM((stretch, plan.groups * channels), BF16),
+            pltpu.VMEM((stretch, plan.groups * channels), BF16),
+            pltpu.VMEM((channels, max(stretch + 128, days + plan.reach)), F32),
             pltpu.VMEM((shifts, channels, plan.reach * channels), F32),
             pltpu.SemaphoreType.DMA((plan.lags,)),
         ],
         compiler_params=pltpu.CompilerParams(vmem_limit_bytes=60 * 1024 * 1024),
-    )(*split(shifted), *split(gathered), counts)
+    )(days_by_device, counts)
 
 
 def factor_and_inverse(gram, width):
@@ -242,11 +262,9 @@
     basis_ref,
     diag_ref,
     off_ref,
-    lh,
-    ll,
+    left,
     zg,
-    zh,
-    zl,
+    right,
     parts,
     q_s,
     z_s,
@@ -266,27 +284,26 @@
 ):
     channels, phases, width = plan.channels, plan.phases, plan.width
     heads, rows, lanes = plan.heads, plan.rows, plan.lanes
-    panel_size, columns = plan.panel_size, plan.columns
+    panel_size, columns, halves = plan.panel_size, plan.columns, plan.halves
     tm, panel = lax.axis_index("tm"), lax.axis_index("panel")
     core, k = tm % 2, tm // 2
+    side, half = panel % 2, panel // 2
     bits = columns.bit_length() - 1
 
-    partners = [("tm", flip(tm, 1 << b)) for b in range(bits + 1)]
-    partners += [("panel", flip(panel, d)) for d in range(1, panel_size)]
+    gram_stages = [[("tm", flip(tm, 1))]]
+    gram_stages.append([("tm", flip(tm, 2 * m)) for m in range(1, columns)])
+    gram_stages.append([("panel", flip(panel, d)) for d in range(1, panel_size)])
+    partners = [partner for stage in gram_stages for partner in stage]
     barrier = pltpu.get_barrier_semaphore()
     for axis, other in partners:
         pl.semaphore_signal(barrier, inc=1, device_id={axis: other}, device_id_type=MESH)
-    gram_partners = [("tm", flip(tm, 1 << b)) for b in range(bits + 1)]
-    gram_partners += [
-        ("panel", flip(panel, 1 << b)) for b in range(panel_size.bit_length() - 1)
-    ]
 
     zero = jnp.zeros((rows, lanes), F32)
     q_s[...] = zero
     v_s[...] = zero
     z_s[...] = x_ref[...]
     guess[...] = jnp.zeros_like(guess)
-    zg[0, k, panel] = x_ref[...]
+    zg[0, k, half] = x_ref[...]
     pl.semaphore_wait(barrier, len(partners))
 
     lane1 = lax.broadcasted_iota(jnp.int32, (width, 2 * width), 1)
@@ -340,21 +357,23 @@
         )
 
     def panel_copy(par, d):
-        slot = zg.at[par, k, panel]
-        return remote(slot, slot, p_send.at[par, d], p_recv.at[par, d], "panel", flip(panel, d))
+        slot = zg.at[par, k, half]
+        other = flip(panel, 2 * d)
+        return remote(slot, slot, p_send.at[par, d], p_recv.at[par, d], "panel", other)
 
     def panel_arrival(par, d):
-        slot = zg.at[par, k, flip(panel, d)]
-        return remote(slot, slot, p_send.at[par, d], p_recv.at[par, d], "panel", flip(panel, d))
+        slot = zg.at[par, k, flip(half, d)]
+        other = flip(panel, 2 * d)
+        return remote(slot, slot, p_send.at[par, d], p_recv.at[par, d], "panel", other)
 
     orders = {}
-    for d in range(panel_size):
+    for d in range(halves):
         order = list(range(bits))
-        orders[d] = order if d < panel_size // 2 else order[::-1]
+        orders[d] = order if d < (halves + 1) // 2 else order[::-1]
 
     def column_copy(par, mask, d, bit):
-        slot = zg.at[par, flip(k, mask), flip(panel, d)]
-        n = (mask ^ (1 << bit)) * panel_size + d
+        slot = zg.at[par, flip(k, mask), flip(half, d)]
+        n = (mask ^ (1 << bit)) * halves + d
         return remote(
             slot, slot, c_send.at[par, n], c_recv.at[par, n], "tm", flip(tm, 2 << bit)
         )
@@ -362,8 +381,8 @@
     def column_arrival(par, mask, d):
         order = orders[d]
         bit = [b for b in order if mask & (1 << b)][-1]
-        slot = zg.at[par, flip(k, mask), flip(panel, d)]
-        n = mask * panel_size + d
+        slot = zg.at[par, flip(k, mask), flip(half, d)]
+        n = mask * halves + d
         return remote(
             slot, slot, c_send.at[par, n], c_recv.at[par, n], "tm", flip(tm, 2 << bit)
         )
@@ -371,29 +390,47 @@
     def last_stage(mask, d):
         return max([s for s, b in enumerate(orders[d]) if mask & (1 << b)], default=-1)
 
-    def gram_copy(par, s):
-        axis, other = gram_partners[s]
-        return remote(
-            g_held.at[par, s], g_got.at[par, s], g_send.at[par, s], g_recv.at[par, s], axis, other
-        )
+    def gram_copies(par, s):
+        first = sum(len(stage) for stage in gram_stages[:s])
+        return [
+            remote(
+                g_held.at[par, s],
+                g_got.at[par, first + n],
+                g_send.at[par, first + n],
+                g_recv.at[par, first + n],
+                axis,
+                other,
+            )
+            for n, (axis, other) in enumerate(gram_stages[s])
+        ]
+
+    def gram_send(par, s):
+        copies = gram_copies(par, s)
+        for copy in copies:
+            copy.start()
+        return copies
 
     def local_gram(par):
-        q, z = q_s[...], z_s[...]
-        first = folded(t_times(q, z))
-        second = folded(t_times(z, z))
+        z = z_s[...]
+        both = t_times(jnp.concatenate([q_s[...], z], axis=1), z)
+        first = folded(both[:lanes])
+        second = folded(both[lanes:])
         g_held[par, 0] = jnp.where(lane1 < width, first, pltpu.roll(second, width, 1))
-        gram_copy(par, 0).start()
-
-    def gram_stage(par, s):
-        copy = gram_copy(par, s)
-        copy.wait_recv()
-        g_held[par, s + 1] = g_held[par, s] + g_got[par, s]
-        copy.wait_send()
-        if s + 1 < len(gram_partners):
-            gram_copy(par, s + 1).start()
+        return gram_send(par, 0)
+
+    def gram_stage(par, s, copies):
+        first = sum(len(stage) for stage in gram_stages[:s])
+        terms = [g_held[par, s]]
+        for n, copy in enumerate(copies):
+            copy.wait_recv()
+            terms.append(g_got[par, first + n])
+        while len(terms) > 1:
+            terms = [terms[n] + terms[n + 1] for n in range(0, len(terms), 2)]
+        g_held[par, s + 1] = terms[0]
+        return gram_send(par, s + 1) if s + 1 < len(gram_stages) else []
 
     def small(par, j):
-        both = g_held[par, len(gram_partners)]
+        both = g_held[par, len(gram_stages)]
         rest = jnp.where(lane1 < width, both, 0.0)
         square = t_times(rest, rest)[:width]
         gram = pltpu.roll(both, width, 1) - square
@@ -404,8 +441,8 @@
         spread_rest = spread(rest)
         spread_r = spread(work)
         spread_l = spread(pltpu.roll(work, width, 1))
-        q = q_s[...]
-        after = z_s[...] - times(q, spread_rest)
+        products = times(jnp.concatenate([q_s[...], v_s[...]], axis=0), spread_rest)
+        after = z_s[...] - products[:rows]
         following = times_t(after, spread_l)
         for p in range(phases):
             block = following[:, (p // 2) * 2 * width :][:, : 2 * width]
@@ -415,49 +452,56 @@
                 basis_ref[j, pl.ds((h * phases + p) * channels, channels), :] = block[
                     h * channels : (h + 1) * channels, :width
                 ]
-        return diag, spread_rest, spread_r, spread_l, following
-
-    def build(own):
+        return diag, products[rows:], spread_r, spread_l, following
+
+    def build(same_core, same_side):
         total = plan.units * channels
-        back = plan.run // phases * channels
-        stride = 2 * back
+        ahead = side if same_side else 3 * side - 1
+        ahead = ahead * heads
+        if not same_core:
+            ahead = ahead + (2 * core - 1) * (plan.run // phases)
+        turn = (total - ahead * channels) % total
+        variant = 2 * int(same_core) + int(same_side)
+        stride = 2 * plan.run // phases * channels
+        piece = heads * channels
         for p in range(phases):
 
             def chunk(c, carry):
                 at = pl.multiple_of(p * channels + c * 16, 16)
-                part = near_ref[pl.ds(at, 16), :]
-                if not own:
-                    part = jnp.where(
-                        core == 1, pltpu.roll(part, total - back, 1), pltpu.roll(part, back, 1)
-                    )
+                part = pltpu.roll(near_ref[pl.ds(at, 16), :], turn, 1)
                 for i in range(1 - phases, plan.lags):
                     if (plan.pad - i - p) % phases:
                         continue
                     u0 = (plan.pad - i - p) // phases
-                    turned = pltpu.roll(part, total - u0 * channels, 1)
-                    pieces = [turned[:, n * stride : n * stride + back] for n in range(columns)]
-                    line = jnp.concatenate(pieces, axis=1)
-                    high = line.astype(BF16)
-                    low = (line - high.astype(F32)).astype(BF16)
                     to = pl.ds(pl.multiple_of((i + phases - 1) * channels + c * 16, 16), 16)
-                    lh[int(own), to, :] = high
-                    ll[int(own), to, :] = low
+                    for h in range(halves):
+                        pieces = []
+                        for n in range(columns):
+                            start = u0 * channels + n * stride + 2 * h * piece
+                            pieces.append(part[:, start : start + piece])
+                        line = jnp.concatenate(pieces, axis=1)
+                        high = line.astype(BF16)
+                        low = (line - high.astype(F32)).astype(BF16)
+                        depth = line.shape[1]
+                        left[variant, h, to, :depth] = high
+                        left[variant, h, to, depth : 2 * depth] = high
+                        left[variant, h, to, 2 * depth :] = low
                 return carry
 
             lax.fori_loop(0, channels // 16, chunk, 0)
 
-    def product(which):
-        high, low = zh[...], zl[...]
-        parts[...] = jnp.dot(lh[which], high, preferred_element_type=F32)
-        parts[...] += jnp.dot(lh[which], low, preferred_element_type=F32)
-        parts[...] += jnp.dot(ll[which], high, preferred_element_type=F32)
+    def add_product(variant, which, first):
+        total = jnp.dot(left[variant, which], right[which], preferred_element_type=F32)
+        parts[variant] = total if first else parts[variant] + total
+
+    def combined(variant):
         lane = lax.broadcasted_iota(jnp.int32, (channels, lanes), 1)
         out = []
         for h in range(heads):
             total = None
             for delta in range(1 - phases, phases):
                 i = h * phases + delta + phases - 1
-                term = parts[i * channels : (i + 1) * channels, :]
+                term = parts[variant, i * channels : (i + 1) * channels, :]
                 if delta:
                     term = pltpu.roll(term, (delta * width) % lanes, 1)
                     if delta > 0:
@@ -474,100 +518,148 @@
             )
         return whole
 
+    def take_in(par, mask, d):
+        column = flip(k, mask)
+        block = zg[par, column, flip(half, d)]
+        high = block.astype(BF16)
+        low = (block - high.astype(F32)).astype(BF16)
+        for n, term in enumerate((high, low, high)):
+            to = pl.ds(pl.multiple_of((n * columns + column) * rows, 16), rows)
+            right[flip(half, d), to, :] = term
+
+    events = [(2.0, "gram", 0), (6.5, "gram", 1), (13.0, "gram", 2), (13.5, "small", 0)]
+    events.append((9.5, "products", 0))
+    for d in range(halves):
+        if d:
+            events.append((7.0 * d, "panel", d))
+        for mask in range(1, columns):
+            if last_stage(mask, d) < bits - 1:
+                hops = bin(mask).count("1")
+                events.append((7.0 * d + 4.5 * hops, "column", (mask, d)))
+    events.sort(key=lambda event: event[0])
+
     def iteration(j, carry):
         par = j % 2
         sends = []
-        for d in range(1, panel_size):
+
+        def forward(mask, d):
+            for bit in orders[d][last_stage(mask, d) + 1 :]:
+                copy = column_copy(par, mask, d, bit)
+                copy.start()
+                sends.append(copy)
+
+        def arrive(mask, d):
+            arrival = column_arrival(par, mask, d) if mask else panel_arrival(par, d)
+            arrival.wait_recv()
+            forward(mask, d)
+            take_in(par, mask, d)
+            arrived.add((mask, d))
+
+        def arrive_half(d):
+            for mask in range(columns):
+                if (mask, d) not in arrived:
+                    arrive(mask, d)
+
+        for d in range(1, halves):
             copy = panel_copy(par, d)
             copy.start()
             sends.append(copy)
-        for bit in orders[0]:
-            copy = column_copy(par, 0, 0, bit)
-            copy.start()
-            sends.append(copy)
-        local_gram(par)
-        stages = list(range(len(gram_partners)))
-
-        def next_stage():
-            if stages:
-                gram_stage(par, stages.pop(0))
-
-        for d in range(1, panel_size):
-            panel_arrival(par, d).wait_recv()
-            for bit in orders[d]:
-                copy = column_copy(par, 0, d, bit)
-                copy.start()
-                sends.append(copy)
-            next_stage()
-        waited = set()
-        for s in range(bits - 1):
-            for d in range(panel_size):
-                for mask in range(1, columns):
-                    if last_stage(mask, d) != s:
-                        continue
-                    column_arrival(par, mask, d).wait_recv()
-                    waited.add((mask, d))
-                    for bit in orders[d][s + 1 :]:
-                        copy = column_copy(par, mask, d, bit)
-                        copy.start()
-                        sends.append(copy)
-                    next_stage()
-        while stages:
-            next_stage()
-        diag, spread_rest, spread_r, spread_l, following = small(par, j)
-        v_part = times(v_s[...], spread_rest)
-        q_r = times_t(q_s[...], spread_r) + times(following, spread(diag))
-        guess[...] = diag
+        forward(0, 0)
 
         @pl.when(j == 0)
         def _():
-            build(False)
-            build(True)
-
-        for mask in range(1, columns):
-            for d in range(panel_size):
-                if (mask, d) not in waited:
-                    column_arrival(par, mask, d).wait_recv()
-        for n in range(columns):
-            for d in range(panel_size):
-                block = zg[par, n, d]
-                high = block.astype(BF16)
-                at = pl.ds((n * panel_size + d) * rows, rows)
-                zh[at, :] = high
-                zl[at, :] = (block - high.astype(F32)).astype(BF16)
-        y_send[par] = product(0)
-        to_other = remote(
-            y_send.at[par], y_recv.at[par], y_sems.at[par, 0], y_sems.at[par, 1], "tm", flip(tm, 1)
+            for same_core in (False, True):
+                for same_side in (False, True):
+                    build(same_core, same_side)
+
+        gram = local_gram(par)
+        sends += gram
+        take_in(par, 0, 0)
+        arrived = {(0, 0)}
+        for _, kind, what in events:
+            if kind == "gram":
+                gram = gram_stage(par, what, gram)
+                sends += gram
+            elif kind == "small":
+                diag, v_part, spread_r, spread_l, following = small(par, j)
+                q_r = times_t(q_s[...], spread_r) + times(following, spread(diag))
+            elif kind == "products":
+                for d in range(halves - 1):
+                    arrive_half(d)
+                    for variant in range(4):
+                        add_product(variant, flip(half, d), d == 0)
+            elif kind == "panel":
+                arrive(0, what)
+            else:
+                arrive(*what)
+        guess[...] = diag
+        last = halves - 1
+        arrive_half(last)
+        across = {}
+
+        def to_core(other_side):
+            variant = 1 - other_side
+            add_product(variant, flip(half, last), last == 0)
+            y_send[par, other_side] = combined(variant)
+            copy = remote(
+                y_send.at[par, other_side],
+                y_recv.at[par, other_side],
+                y_sems.at[par, other_side],
+                y_sems.at[par, 2 + other_side],
+                "tm",
+                flip(tm, 1),
+            )
+            copy.start()
+            across[other_side] = copy
+
+        to_core(1)
+        add_product(2, flip(half, last), last == 0)
+        near_side = combined(2)
+        across[1].wait_recv()
+        y_send[par, 2] = near_side + y_recv[par, 1]
+        over = remote(
+            y_send.at[par, 2],
+            y_recv.at[par, 2],
+            y_sems.at[par, 4],
+            y_sems.at[par, 5],
+            "panel",
+            flip(panel, 1),
         )
-        to_other.start()
-        mine = product(1)
-        to_other.wait_recv()
-        y = mine + y_recv[par]
-        v = times_t(y - v_part, spread_l)
+        over.start()
+        to_core(0)
+        add_product(3, flip(half, last), last == 0)
+        mine = combined(3) - v_part
+        across[0].wait_recv()
+        mine = mine + y_recv[par, 0]
+        over.wait_recv()
+        v = times_t(mine + y_recv[par, 2], spread_l)
         z = v - q_r
         v_s[...] = v
         z_s[...] = z
         q_s[...] = following
-        zg[1 - par, k, panel] = z
-        for copy in sends:
+        zg[1 - par, k, half] = z
+        for copy in sends + [across[0], across[1], over]:
             copy.wait_send()
-        to_other.wait_send()
         return carry
 
     lax.fori_loop(0, ITERS, iteration, 0)
     par = ITERS % 2
-    local_gram(par)
-    for s in range(len(gram_partners)):
-        gram_stage(par, s)
+    gram = local_gram(par)
+    sends = list(gram)
+    for s in range(len(gram_stages)):
+        gram = gram_stage(par, s, gram)
+        sends += gram
     small(par, ITERS)
+    for copy in sends:
+        copy.wait_send()
 
 
 def lanczos(plan, near, packed):
     channels, phases, width = plan.channels, plan.phases, plan.width
     rows, lanes = plan.rows, plan.lanes
-    blocks = plan.columns * plan.panel_size
+    blocks = plan.columns * plan.halves
     groups = (plan.lags + phases - 1) * channels
-    stages = (plan.tm_size * plan.panel_size).bit_length() - 1
+    others = plan.columns + plan.panel_size - 1
     block = (rows, lanes)
     pair = (width, 2 * width)
     dma = pltpu.SemaphoreType.DMA
@@ -581,27 +673,25 @@
         in_specs=[VMEM] * 2,
         out_specs=(VMEM,) * 3,
         scratch_shapes=[
-            pltpu.VMEM((2, groups, blocks * rows), BF16),
-            pltpu.VMEM((2, groups, blocks * rows), BF16),
-            pltpu.VMEM((2, plan.columns, plan.panel_size) + block, F32),
-            pltpu.VMEM((blocks * rows, lanes), BF16),
-            pltpu.VMEM((blocks * rows, lanes), BF16),
-            pltpu.VMEM((groups, lanes), F32),
+            pltpu.VMEM((4, plan.halves, groups, 3 * plan.columns * rows), BF16),
+            pltpu.VMEM((2, plan.columns, plan.halves) + block, F32),
+            pltpu.VMEM((plan.halves, 3 * plan.columns * rows, lanes), BF16),
+            pltpu.VMEM((4, groups, lanes), F32),
             pltpu.VMEM(block, F32),
             pltpu.VMEM(block, F32),
             pltpu.VMEM(block, F32),
             pltpu.VMEM(pair, F32),
-            pltpu.VMEM((2,) + block, F32),
-            pltpu.VMEM((2,) + block, F32),
-            pltpu.VMEM((2, stages + 1) + pair, F32),
-            pltpu.VMEM((2, stages) + pair, F32),
-            dma((2, plan.panel_size)),
-            dma((2, plan.panel_size)),
+            pltpu.VMEM((2, 3) + block, F32),
+            pltpu.VMEM((2, 3) + block, F32),
+            pltpu.VMEM((2, 4) + pair, F32),
+            pltpu.VMEM((2, others) + pair, F32),
+            dma((2, plan.halves)),
+            dma((2, plan.halves)),
             dma((2, blocks)),
-            dma((2, blocks * max(1, plan.columns.bit_length()))),
-            dma((2, stages)),
-            dma((2, stages)),
-            dma((2, 2)),
+            dma((2, blocks)),
+            dma((2, others)),
+            dma((2, others)),
+            dma((2, 6)),
         ],
         compiler_params=pltpu.CompilerParams(
             collective_id=1, has_side_effects=True, vmem_limit_bytes=60 * 1024 * 1024

time: 365 us -> 293 us (0.80)
  Pallas kernels: 331 us -> 283 us
  local copies, waits for them, and re-layouts: 25.6 us -> 8.16 us
  other arithmetic: 6.94 us -> 0.7 us
    pallas_call x1, Pallas kernels: 282 us -> 227 us  [lanczos(): pl.pallas_call(lambda *refs: lanczos_kernel(plan, *refs), out_shape=(jax....]
    concatenate x1 -> x0, local copies, waits for them, and re-layouts: 9.16 us -> none  [covariance_rows(): jnp.concatenate([near_days[phases * g:phases * g + stretch] for g in rang...]
    slice x1 -> x0, local copies, waits for them, and re-layouts: 8.69 us -> none  [covariance_rows(): near_days[phases * g:phases * g + stretch]]
    pallas_call x1, Pallas kernels: 38.3 us -> 45.9 us  [covariance_rows(): pl.pallas_call(lambda *refs: covariance_kernel(plan, *refs), out_shape=(j...]
    convert_element_type x2 -> x0, other arithmetic: 6.25 us -> none  [split(): return (high.astype(BF16), (array - high).astype(BF16))]
where the time goes in v2:
time: 293 us
  Pallas kernels  283 us (97%)
  local copies, waits for them, and re-layouts  8.16 us (3%)
    pallas_call x1, Pallas kernels, lanczos(): pl.pallas_call(lambda *refs: lanczos_kernel(plan, *refs), out_shape=(jax....  227 us
    pallas_call x1, Pallas kernels, covariance_rows(): pl.pallas_call(lambda *refs: covariance_kernel(plan, *refs), out_shape=(j...  45.9 us
    pallas_call x1, Pallas kernels, all_days(): pl.pallas_call(lambda *refs: series_kernel(size, *refs), out_shape=jax.Sh...  10.9 us

profile of v2, /device:TPU:0, one launch (start us, length us, event | category | flops | bytes accessed | tf_op | source)
XLA Modules:
  0.0 292.9 jit_solution(12240202222092987291)
XLA Ops:
  0.7 0.7 subtract_convert_fusion.refs_1_
  1.4 1.1 copy.8
  2.4 0.1 copy.9
  2.5 0.9 reshape.30.refs_1_
  3.4 10.9 %shard_map.57.refs_0_ = f32[8,48,256]{2,1,0:T(8,128)} custom-call(f32[48,256]{1,0:T(8,128)} %refs_0_.1), custom_call_target="tpu_custom_call" | custom-call | tf_op jit(solution)/shard_map/pallas_call | solution.py:87
  14.3 45.9 %shard_map.58 = (f32[192,6144]{1,0:T(8,128)}, f32[576,18432]{1,0:T(8,128)}) custom-call(f32[8,48,256]{2,1,0:T(8,128)} %shard_map.57.refs_0_, f32[4,6144]{1,0:T(4,128)} %subtract_convert_fusion.refs_1_), custom_call_target="tpu_custom_call" | custom-call | tf_op jit(solution)/shard_map/pallas_call | solution.py:223
  60.1 226.6 %shard_map.59 = (f32[7,576,64]{2,1,0:T(8,128)}, f32[7,64,64]{2,1,0:T(8,128)}, f32[7,64,64]{2,1,0:T(8,128)}) custom-call(f32[192,6144]{1,0:T(8,128)} %get-tuple-element.10.refs_0_, f32[144,256]{1,0:T(8,128)} %reshape.30.refs_1_), custom_call_target="tpu_custom_call" | custom-call | tf_op jit(solution)/shard_map/pallas_call | solution.py:666
  286.8 2.8 copy.10
  289.6 1.6 slice.3
  291.2 1.6 copy.12
  (1 shorter events, 0.0 us)

commit v3 on v2

--- a/solution.py
+++ b/solution.py
@@ -43,6 +43,7 @@
         self.reach = round_up(self.reach, self.groups * self.phases)
         self.units = self.reach // self.phases
         self.steps = self.units // self.groups
+        self.together = 2 if self.steps % 2 == 0 and 2 * self.groups * channels <= 768 else 1
         self.depth = days + 128
         self.heads = self.lags // self.phases
         self.rows = self.heads * channels
@@ -99,7 +100,7 @@
 
 
 def covariance_kernel(
-    plan, d_ref, n_ref, near_ref, c_ref, xh_ref, xl_ref, gh_ref, gl_ref, moved, wide, sem
+    plan, d_ref, n_ref, near_ref, c_ref, xh_ref, xl_ref, gh_ref, gl_ref, moved, woven, wide, sem
 ):
     channels, phases = plan.channels, plan.phases
     unit = plan.groups * channels
@@ -129,9 +130,55 @@
         return carry
 
     lax.fori_loop(0, gh_ref.shape[0] // 128, transpose, 0)
-    together = max(g for g in (1, 2) if plan.steps % g == 0 and g * unit <= 768)
+    together = plan.together
+
+    span = together * unit * phases
+    core = tm % 2
+    jump = plan.run * channels
+    behind = -(-plan.pad * channels // span)
+    pieces = M * channels // span
+    rows_of = []
+    shifts = {}
+    for i in range(plan.lags):
+        first = (plan.pad - i) * channels
+        if jump % 128:
+            first = first - jump * core
+            start = (first - 1) // 128 * 128
+            shift = first - start
+        else:
+            start = (first - 1) // 128 * 128
+            shift = first - start
+            start = start - jump * core
+        slot = shifts.setdefault((plan.pad - i) * channels % 128, (len(shifts), shift))[0]
+        rows_of.append((slot, start))
+    woven[...] = jnp.zeros(woven.shape, F32)
+
+    def row_copy(i, q):
+        slot, start = rows_of[i]
+        at = pl.multiple_of(start + 128 + span * q, 128)
+        to = pl.multiple_of(span * q, 128)
+        return pltpu.make_async_copy(
+            wide.at[slot, :, pl.ds(at, span)],
+            c_ref.at[pl.ds(i * channels, channels), pl.ds(to, span)],
+            sem.at[i, q],
+        )
+
+    def turn(step):
+        to = pl.ds(pl.multiple_of(step * span, 128), span)
+        for group in range(channels // 8):
+            rows = slice(group * 8, group * 8 + 8)
+            whole = woven[rows, :]
+            for slot, shift in shifts.values():
+                wide[slot, rows, to] = pltpu.roll(whole, span + 128 - shift, 1)[:, :span]
+
+    def send_rows(step):
+        @pl.when((step >= behind) & (step < behind + pieces))
+        def _():
+            for i in range(plan.lags):
+                row_copy(i, step - behind).start()
 
     def product(step, carry):
+        turn(jnp.maximum(step - 1, 0))
         pieces_h, pieces_l = [], []
         for g in range(together):
             start = pl.multiple_of((step * together + g) * plan.groups * phases, 16)
@@ -147,69 +194,28 @@
         for p in range(phases):
             rows = slice(p * channels, (p + 1) * channels)
             near_ref[rows, at] = total[rows] / counts[p : p + 1]
+
+        woven[:, :128] = woven[:, span:]
+        for t in range(together):
+            start = pl.multiple_of((step * together + t) * unit, 128)
+            block = near_ref[:, pl.ds(start, unit)]
+            parts = [
+                block[p * channels : (p + 1) * channels, g * channels : (g + 1) * channels]
+                for g in range(plan.groups)
+                for p in range(phases)
+            ]
+            to = 128 + t * unit * phases
+            woven[:, to : to + unit * phases] = jnp.concatenate(parts, axis=1)
+        send_rows(step - 1)
         return carry
 
-    lax.fori_loop(0, plan.steps // together, product, 0)
-
-    def weave(step, carry):
-        block = near_ref[:, pl.ds(pl.multiple_of(step * unit, 128), unit)]
-        pieces = [
-            block[p * channels : (p + 1) * channels, g * channels : (g + 1) * channels]
-            for g in range(plan.groups)
-            for p in range(phases)
-        ]
-        at = pl.ds(pl.multiple_of(step * unit * phases, 128), unit * phases)
-        wide[0, :, at] = jnp.concatenate(pieces, axis=1)
-        return carry
-
-    lax.fori_loop(0, plan.steps, weave, 0)
-
-    total = plan.reach * channels
-    core = lax.axis_index("tm") % 2
-    jump = plan.run * channels
-    if jump % 128:
-
-        def choose(group, carry):
-            rows = pl.ds(pl.multiple_of(group * 8, 8), 8)
-            whole = wide[0, rows, :]
-            back = pltpu.roll(whole, jump, 1)
-            wide[0, rows, :] = jnp.where(core == 1, back, whole)
-            return carry
-
-        lax.fori_loop(0, channels // 8, choose, 0)
-    slots = {}
-    order = []
-    for i in range(plan.lags):
-        shift = ((plan.pad - i) * channels) % 128
-        if shift not in slots:
-            slots[shift] = len(slots)
-    slots = {s: n for n, s in enumerate(sorted(slots))}
-    copies = []
-    for shift, slot in slots.items():
-        if slot > 0:
-
-            def turn(group, carry):
-                rows = pl.ds(pl.multiple_of(group * 8, 8), 8)
-                wide[slot, rows, :] = pltpu.roll(wide[0, rows, :], total - shift, 1)
-                return carry
-
-            lax.fori_loop(0, channels // 8, turn, 0)
+    last = plan.steps // together
+    lax.fori_loop(0, last, product, 0)
+    turn(last - 1)
+    send_rows(last - 1)
+    for q in range(pieces):
         for i in range(plan.lags):
-            first = (plan.pad - i) * channels
-            if first % 128 != shift:
-                continue
-            start = first - shift
-            if jump % 128 == 0:
-                start = pl.multiple_of(start - jump * core, 128)
-            copy = pltpu.make_async_copy(
-                wide.at[slot, :, pl.ds(start, M * channels)],
-                c_ref.at[pl.ds(i * channels, channels), :],
-                sem.at[i],
-            )
-            copy.start()
-            copies.append(copy)
-    for copy in copies:
-        copy.wait()
+            row_copy(i, q).wait()
 
 
 def covariance_rows(plan, days_by_device):
@@ -219,7 +225,8 @@
     lag = base + jnp.arange(plan.units * channels) // channels * phases
     lag = lag[None, :] + jnp.arange(phases)[:, None]
     counts = (days - jnp.abs(lag)).astype(F32)
-    shifts = len({((plan.pad - i) * channels) % 128 for i in range(plan.lags)} | {0})
+    shifts = len({(plan.pad - i) * channels % 128 for i in range(plan.lags)})
+    span = plan.together * plan.groups * phases * channels
     return pl.pallas_call(
         lambda *refs: covariance_kernel(plan, *refs),
         out_shape=(
@@ -234,8 +241,9 @@
             pltpu.VMEM((stretch, plan.groups * channels), BF16),
             pltpu.VMEM((stretch, plan.groups * channels), BF16),
             pltpu.VMEM((channels, max(stretch + 128, days + plan.reach)), F32),
+            pltpu.VMEM((channels, span + 128), F32),
             pltpu.VMEM((shifts, channels, plan.reach * channels), F32),
-            pltpu.SemaphoreType.DMA((plan.lags,)),
+            pltpu.SemaphoreType.DMA((plan.lags, M * channels // span)),
         ],
         compiler_params=pltpu.CompilerParams(vmem_limit_bytes=60 * 1024 * 1024),
     )(days_by_device, counts)
@@ -529,6 +537,10 @@
 
     events = [(2.0, "gram", 0), (6.5, "gram", 1), (13.0, "gram", 2), (13.5, "small", 0)]
     events.append((9.5, "products", 0))
+    events.append((0.5, "build", (False, False)))
+    events.append((2.5, "build", (False, True)))
+    events.append((7.1, "build", (True, False)))
+    events.append((7.2, "build", (True, True)))
     for d in range(halves):
         if d:
             events.append((7.0 * d, "panel", d))
@@ -565,12 +577,6 @@
             copy.start()
             sends.append(copy)
         forward(0, 0)
-
-        @pl.when(j == 0)
-        def _():
-            for same_core in (False, True):
-                for same_side in (False, True):
-                    build(same_core, same_side)
 
         gram = local_gram(par)
         sends += gram
@@ -583,6 +589,12 @@
             elif kind == "small":
                 diag, v_part, spread_r, spread_l, following = small(par, j)
                 q_r = times_t(q_s[...], spread_r) + times(following, spread(diag))
+            elif kind == "build":
+
+                @pl.when(j == 0)
+                def _():
+                    build(*what)
+
             elif kind == "products":
                 for d in range(halves - 1):
                     arrive_half(d)

time: 293 us -> 274 us (0.935)
  Pallas kernels: 283 us -> 264 us
    pallas_call x1, Pallas kernels: 45.9 us -> 35.5 us  [covariance_rows(): pl.pallas_call(lambda *refs: covariance_kernel(plan, *refs), out_shape=(j...]
    pallas_call x1, Pallas kernels: 227 us -> 217 us  [lanczos(): pl.pallas_call(lambda *refs: lanczos_kernel(plan, *refs), out_shape=(jax....]
where the time goes in v3:
time: 274 us; the launch traced here: 273 us
  Pallas kernels  264 us (96%)
  local copies, waits for them, and re-layouts  8.16 us (3%)
    pallas_call x1, Pallas kernels, lanczos(): pl.pallas_call(lambda *refs: lanczos_kernel(plan, *refs), out_shape=(jax....  217 us
    pallas_call x1, Pallas kernels, covariance_rows(): pl.pallas_call(lambda *refs: covariance_kernel(plan, *refs), out_shape=(j...  35.5 us
    pallas_call x1, Pallas kernels, all_days(): pl.pallas_call(lambda *refs: series_kernel(size, *refs), out_shape=jax.Sh...  10.9 us
    unnamed x3, local copies, waits for them, and re-layouts  5.55 us

profile of v3, /device:TPU:0, one launch (start us, length us, event | category | flops | bytes accessed | tf_op | source)
XLA Modules:
  0.0 273.3 jit_solution(5863285477882844852)
XLA Ops:
  0.7 0.7 subtract_convert_fusion.refs_1_
  1.4 1.1 copy.8
  2.4 0.1 copy.9
  2.5 0.9 reshape.30.refs_1_
  3.4 10.9 %shard_map.57.refs_0_ = f32[8,48,256]{2,1,0:T(8,128)} custom-call(f32[48,256]{1,0:T(8,128)} %refs_0_.1), custom_call_target="tpu_custom_call" | custom-call | tf_op jit(solution)/shard_map/pallas_call | solution.py:88
  14.3 35.5 %shard_map.58 = (f32[192,6144]{1,0:T(8,128)}, f32[576,18432]{1,0:T(8,128)}) custom-call(f32[8,48,256]{2,1,0:T(8,128)} %shard_map.57.refs_0_, f32[4,6144]{1,0:T(4,128)} %subtract_convert_fusion.refs_1_), custom_call_target="tpu_custom_call" | custom-call | tf_op jit(solution)/shard_map/pallas_call | solution.py:230
  49.8 217.4 %shard_map.59 = (f32[7,576,64]{2,1,0:T(8,128)}, f32[7,64,64]{2,1,0:T(8,128)}, f32[7,64,64]{2,1,0:T(8,128)}) custom-call(f32[192,6144]{1,0:T(8,128)} %get-tuple-element.10.refs_0_, f32[144,256]{1,0:T(8,128)} %reshape.30.refs_1_), custom_call_target="tpu_custom_call" | custom-call | tf_op jit(solution)/shard_map/pallas_call | solution.py:678
  267.2 2.8 %copy.10 = f32[7,576,64]{1,2,0:T(8,128)} copy(f32[7,576,64]{2,1,0:T(8,128)} %get-tuple-element.19) | data formatting | bytes 2064384
  270.1 1.6 slice.3
  271.7 1.6 copy.12
  (1 shorter events, 0.0 us)
